TPU v7x, 32 devices: a whole 2x2x4 slice. The times are simulated.
32 devices in a mesh: grid: 8 (over z, x), orb: 4 (over y, core).
Axes of the slice: x: 2, y: 2, z: 4, core: 2. Of those that a mesh axis runs over, the one named last changes fastest.
Arguments:
- orbitals: bfloat16 [1800, 65536], P('orb', 'grid'), may hold values from -0.5 to 1.5
- pivots: int32 [3, 96], replicated, may hold values from 0 to 65535, as said below
Outputs:
- cholesky_factor: float32 [65536, 288], P(('grid', 'orb'))
- residual_diagonal: float32 [65536], P(('grid', 'orb'))
- diagonal_peaks: float32 [3], replicated
Inputs may be any that keep to these rules, and one draw needn't show every extreme that they name: `pivots`: all 3 x 96 pivot indices are distinct grid points.
All inputs are finite; a program needn't handle non-finite values.
Results may differ from a plain program's by a relative error of at most 0.0003.
Values may be sent and summed in bfloat16 or wider, within the bound.
A program may use at most 64 MiB of HBM per device.

v0:
```python
import jax
import jax.numpy as jnp
from jax import lax
from jax.sharding import PartitionSpec as P

ORB = 1800


def pick_columns(values, index, base, count):
    local = index - base
    inside = (local >= 0) & (local < count)
    taken = jnp.take(values, jnp.clip(local, 0, count - 1), axis=1)
    return jnp.where(inside[None, :], taken, jnp.zeros_like(taken))


def contract_first(left, right):
    return lax.dot_general(
        left, right, (((0,), (0,)), ((), ())), preferred_element_type=jnp.float32
    )


def on_device(orbitals, pivots):
    rows = orbitals.shape[1]
    groups = lax.axis_size("orb")
    share = rows // groups
    sections = pivots.shape[0]
    count = pivots.shape[1]
    total_rank = sections * count
    grid_base = lax.axis_index("grid") * rows
    squares = lax.psum_scatter(
        jnp.sum(jnp.square(orbitals.astype(jnp.float32)), axis=0),
        "orb",
        scatter_dimension=0,
        tiled=True,
    )
    diagonal = jnp.square(squares / ORB)
    factor = jnp.zeros((share, total_rank), jnp.float32)
    flat = pivots.reshape(total_rank)
    local_pivots = lax.psum(
        pick_columns(orbitals, flat, grid_base, rows).astype(jnp.float32).astype(jnp.bfloat16),
        "grid",
    )
    whole = lax.all_gather(local_pivots, "orb", axis=0, tiled=True)
    pivot_pairs = contract_first(whole, whole)
    pivot_factor = jnp.zeros((total_rank, total_rank), jnp.float32)
    peaks = []
    for section in range(sections):
        lead = section * count
        sampled_here = lax.slice_in_dim(local_pivots, lead, lead + count, axis=1)
        known = lax.slice_in_dim(pivot_factor, lead, lead + count, axis=0)
        pair = lax.slice_in_dim(
            lax.slice_in_dim(pivot_pairs, lead, lead + count, axis=0), lead, lead + count, axis=1
        )

        def product(start, length, picked=sampled_here):
            return contract_first(orbitals, picked)

        inner = lax.psum_scatter(
            product(jnp.int32(0), share * lax.axis_size("orb")),
            "orb",
            scatter_dimension=0,
            tiled=True,
        )
        block = jnp.square(pair / ORB) - jnp.dot(known, known.T, precision=lax.Precision.HIGHEST)
        columns = jnp.square(inner / ORB) - jnp.dot(
            factor, known.T, precision=lax.Precision.HIGHEST
        )
        lower = jnp.linalg.cholesky(block)
        fresh = jax.scipy.linalg.solve_triangular(lower, columns.T, lower=True).T
        factor = factor.at[:, lead : lead + count].set(fresh)
        pivot_columns = jnp.square(
            lax.slice_in_dim(pivot_pairs, lead, lead + count, axis=1) / ORB
        ) - jnp.dot(pivot_factor, known.T, precision=lax.Precision.HIGHEST)
        pivot_fresh = jax.scipy.linalg.solve_triangular(lower, pivot_columns.T, lower=True).T
        pivot_factor = pivot_factor.at[:, lead : lead + count].set(pivot_fresh)
        diagonal = diagonal - jnp.sum(fresh * fresh, axis=1)
        peaks.append(lax.pmax(jnp.max(diagonal), ("grid", "orb")))
    peak_values = jnp.stack(peaks)
    return (factor, diagonal, peak_values)


def solution(mesh):
    in_specs = (P("orb", "grid"), P())
    out_specs = (P(("grid", "orb"), None), P(("grid", "orb")), P())
    return jax.shard_map(
        on_device, mesh=mesh, in_specs=in_specs, out_specs=out_specs, check_vma=False
    )
```

profile of v0, /device:TPU:0, one launch (start us, length us, event | category | flops | bytes accessed | tf_op | source)
XLA Modules:
  0.0 281.3 jit_solution(3974365267938279486)
XLA Ops:
  8.8 11.6 %copy.26 = bf16[450,8192]{0,1:T(8,128)(2,1)} copy(bf16[450,8192]{1,0:T(8,128)(2,1)} %param.17) | data formatting | bytes 14745600 | tf_op args[0]
  20.5 6.5 %gather_fusion = bf16[288,450]{1,0:T(8,128)(2,1)S(1)} fusion(bf16[450,8192]{0,1:T(8,128)(2,1)} %copy.26, s32[1024]{0:T(1024)S(1)} %pad_clamp_fusion), kind=kCustom, calls=%fused_computation | custom fusion | bytes 519552 | tf_op jit(solution)/shard_map/jit(_take)/gather | solution.py:12
  27.0 0.9 select_bitcast_fusion.1
  27.9 74.2 %all-reduce.6.cloned.1.call-done = bf16[450,288]{0,1:T(8,128)(2,1)} async-done(((bf16[450,288]{0,1:T(8,128)(2,1)}), bf16[450,288]{0,1:T(8,128)(2,1)}) %all-reduce.6.cloned.1.call-update) | async-done | bytes 259216 | tf_op jit(solution)/shard_map/psum | solution.py:39
  102.1 6.3 %convolution_bitcast_fusion.2 = f32[8192,96]{0,1:T(8,128)} fusion(bf16[450,8192]{1,0:T(8,128)(2,1)} %param.17, bf16[450,288]{0,1:T(8,128)(2,1)} %all-reduce.6.cloned.1.call-done), kind=kOutput, calls=%fused_computation.4 | convolution fusion | flops 707788800 | bytes 10715136 | tf_op jit(solution)/shard_map/dot_general | solution.py:17
  108.5 0.9 copy-done.2
  109.4 6.4 %convolution_bitcast_fusion.1 = f32[8192,96]{0,1:T(8,128)} fusion(bf16[450,8192]{1,0:T(8,128)(2,1)} %param.17, bf16[450,288]{0,1:T(8,128)(2,1)S(1)} %copy-done.2), kind=kOutput, calls=%fused_computation.3 | convolution fusion | flops 707788800 | bytes 10616832 | tf_op jit(solution)/shard_map/dot_general | solution.py:17
  115.8 6.6 %convolution_bitcast_fusion = f32[8192,96]{0,1:T(8,128)} fusion(bf16[450,8192]{1,0:T(8,128)(2,1)} %param.17, bf16[450,288]{0,1:T(8,128)(2,1)S(1)} %copy-done.2), kind=kOutput, calls=%fused_computation.2 | convolution fusion | flops 707788800 | bytes 10616832 | tf_op jit(solution)/shard_map/dot_general | solution.py:17
  125.7 4.8 %multiply_reduce_fusion = f32[8192]{0:T(1024)S(1)} fusion(bf16[450,8192]{1,0:T(8,128)(2,1)} %param.17), kind=kLoop, calls=%fused_computation.1 | loop fusion | flops 11051008 | bytes 7405568 | tf_op jit(solution)/shard_map/reduce_sum | solution.py:31
  130.5 12.2 %all-reduce.2 = f32[8192]{0:T(1024)S(1)} all-reduce(f32[8192]{0:T(1024)S(1)} %multiply_reduce_fusion), channel_id=5, replica_groups=mesh['grid'=8,'orb'=4] {'orb'}, use_global_device_ids=true, to_apply=%region_9.13.clone | all-reduce | flops 8192 | bytes 65536
  142.7 10.8 %all-gather = bf16[4,450,288]{1,2,0:T(8,128)(2,1)S(1)} all-gather(bf16[1,450,288]{1,2,0:T(8,128)(2,1)S(1)} %bitcast.91), channel_id=1, replica_groups=mesh['grid'=8,'orb'=4] {'orb'}, dimensions={0}, use_global_device_ids=true | all-gather | bytes 1296000 | tf_op jit(solution)/shard_map/all_gather | solution.py:43
  153.4 0.9 copy.27
  154.3 1.6 reshape.196
  155.9 0.8 fusion.54
  157.3 8.8 %cholesky.59 = f32[96,96]{1,0:T(8,128)S(1)} custom-call(f32[96,96]{1,0:T(8,128)S(1)} %fusion.36), custom_call_target="Cholesky" | custom-call | tf_op jit(solution)/shard_map/jit(cholesky)/cholesky | solution.py:68
  167.4 7.4 %custom-call.11 = f32[1,96,96]{1,2,0:T(8,128)S(1)} custom-call(f32[1,96,96]{2,1,0:T(8,128)S(1)} %fusion.25), custom_call_target="InvertDiagBlocksLowerTriangular" | custom-call | tf_op jit(solution)/shard_map/jit(_solve_triangular)/triangular_solve | solution.py:69
  174.8 1.0 fusion.5
  176.4 8.8 %cholesky.70 = f32[96,96]{1,0:T(8,128)S(1)} custom-call(f32[96,96]{1,0:T(8,128)S(1)} %fusion.33), custom_call_target="Cholesky" | custom-call | tf_op jit(solution)/shard_map/jit(cholesky)/cholesky | solution.py:68
  186.5 7.4 %custom-call.13 = f32[1,96,96]{1,2,0:T(8,128)S(1)} custom-call(f32[1,96,96]{2,1,0:T(8,128)S(1)} %fusion.26), custom_call_target="InvertDiagBlocksLowerTriangular" | custom-call | tf_op jit(solution)/shard_map/jit(_solve_triangular)/triangular_solve | solution.py:69
  194.6 1.0 fusion.4
  196.3 8.9 %cholesky.81 = f32[96,96]{1,0:T(8,128)S(1)} custom-call(f32[96,96]{1,0:T(8,128)S(1)} %fusion.29), custom_call_target="Cholesky" | custom-call | tf_op jit(solution)/shard_map/jit(cholesky)/cholesky | solution.py:68
  206.5 7.4 %custom-call.15 = f32[1,96,96]{1,2,0:T(8,128)S(1)} custom-call(f32[1,96,96]{2,1,0:T(8,128)S(1)} %fusion.27), custom_call_target="InvertDiagBlocksLowerTriangular" | custom-call | tf_op jit(solution)/shard_map/jit(_solve_triangular)/triangular_solve | solution.py:69
  213.9 2.6 multiply_reduce_fusion.3
  216.9 2.3 fusion.1
  219.2 1.5 bitcast_dynamic-update-slice_fusion
  220.8 5.8 %reduce-scatter.8.cloned.1.call-done = f32[2048,96]{0,1:T(8,128)} async-done(((f32[8192,96]{0,1:T(8,128)}), f32[2048,96]{0,1:T(8,128)}) %reduce-scatter.8.cloned.1.call-update) | async-done | bytes 786448 | tf_op jit(solution)/shard_map/reduce_scatter | solution.py:58
  226.5 3.3 %fusion = f32[96,2048]{1,0:T(8,128)S(1)} fusion(f32[2048,288]{0,1:T(8,128)S(1)} %get-tuple-element.81, f32[2048,96]{0,1:T(8,128)} %reduce-scatter.8.cloned.1.call-done, f32[288,288]{0,1:T(8,128)} %copy-done.1), kind=kOutput, calls=%fused_computation.7 | convolution fusion | flops 680067072 | bytes 4079616 | tf_op jit(solution)/shard_map/dot_general | solution.py:65
  229.9 0.9 multiply_reduce_fusion.1
  230.7 0.8 fusion.46
  231.5 1.2 fusion.48
  232.7 39.6 %all-reduce.3 = (f32[1]{0:T(128)}, f32[1]{0:T(128)}, f32[1]{0:T(128)}) all-reduce(f32[1]{0:T(128)} %bitcast.30, f32[1]{0:T(128)} %bitcast.29, f32[1]{0:T(128)} %bitcast.28), channel_id=1, replica_groups=mesh['grid'=8,'orb'=4] {'grid','orb'}, use_global_device_ids=true, to_apply=%region_18.22 | all-reduce | flops 3 | bytes 24 | tf_op jit(solution)/shard_map/pmax | solution.py:77
  272.3 2.5 pad_maximum_fusion
  (54 shorter events, 11.2 us)
Async XLA Ops:
  7.2 94.9 %all-reduce.6.cloned.1.call-start = ((), (), s32[]{:S(2)}) async-start(), calls=%async_computation.3 | async-start | bytes 589824 | tf_op jit(solution)/shard_map/psum | solution.py:39
  27.9 186.0 %reduce-scatter.4.cloned.1.call-start = ((), (), s32[]{:S(2)}) async-start(), calls=%async_computation.4 | async-start | bytes 3932160 | tf_op jit(solution)/shard_map/reduce_scatter | solution.py:58
  108.4 1.0 copy-start.2
  108.4 108.4 %reduce-scatter.6.cloned.1.call-start = ((), (), s32[]{:S(2)}) async-start(), calls=%async_computation.5 | async-start | bytes 3932160 | tf_op jit(solution)/shard_map/reduce_scatter | solution.py:58
  115.8 110.8 %reduce-scatter.8.cloned.1.call-start = ((), (), s32[]{:S(2)}) async-start(), calls=%async_computation.6 | async-start | bytes 3932160 | tf_op jit(solution)/shard_map/reduce_scatter | solution.py:58
  122.5 0.7 copy-start.3
  195.6 21.0 %copy-start.1 = (f32[288,288]{0,1:T(8,128)}, f32[288,288]{0,1:T(8,128)S(1)}, u32[]{:S(2)}) copy-start(f32[288,288]{0,1:T(8,128)S(1)} %fusion.4) | copy-start | bytes 995332
  230.7 44.1 %copy-start = (f32[2048,288]{0,1:T(8,128)}, f32[2048,288]{0,1:T(8,128)S(1)}, u32[]{:S(2)}) copy-start(f32[2048,288]{0,1:T(8,128)S(1)} %get-tuple-element.77) | copy-start | bytes 7077892
Sparse Core Ops, SparseCore 0:
  28.0 74.0 all-reduce.5
  108.6 37.2 reduce-scatter.3
  148.4 37.8 reduce-scatter.5
  188.7 37.7 reduce-scatter.7
where the time goes:
time: 282 us; the launch traced here: 281 us
  waiting for transfers between devices  80.1 us (28%)
  other arithmetic  65.5 us (23%)
  blocking collectives  62.5 us (22%)
  matrix products  34.5 us (12%)
  local copies, waits for them, and re-layouts  23.8 us (8%)
  between operations  14.8 us (5%)
    psum x1, waiting for transfers between devices, on_device(): lax.psum(pick_columns(orbitals, flat, grid_base, rows).astype(jnp.float32...  74.2 us
    pmax x1, blocking collectives, on_device(): peaks.append(lax.pmax(jnp.max(diagonal), ('grid', 'orb')))  39.6 us
    another operation x9, other arithmetic, on_device(): lower = jnp.linalg.cholesky(block)  28.5 us
    another operation x6, other arithmetic, on_device(): fresh = jax.scipy.linalg.solve_triangular(lower, columns.T, lower=True).T  24 us
    dot_general x4, matrix products, contract_first(): lax.dot_general(left, right, (((0,), (0,)), ((), ())), preferred_element_...  20.1 us
    unnamed x14, local copies, waits for them, and re-layouts  15.5 us
    unnamed x1, blocking collectives  12.2 us
    all_gather x1, blocking collectives, on_device(): whole = lax.all_gather(local_pivots, 'orb', axis=0, tiled=True)  10.8 us
  transfers between devices with their start and end apart: 4, of which 2 were waited for; matrix products, arithmetic and copies ran while one was open for 31% of the time, Pallas kernels for 0%

commit v1 on v0

--- a/solution.py
+++ b/solution.py
@@ -36,9 +36,12 @@
     diagonal = jnp.square(squares / ORB)
     factor = jnp.zeros((share, total_rank), jnp.float32)
     flat = pivots.reshape(total_rank)
-    local_pivots = lax.psum(
-        pick_columns(orbitals, flat, grid_base, rows).astype(jnp.float32).astype(jnp.bfloat16),
-        "grid",
+    local_pivots = jnp.sum(
+        lax.all_gather(
+            pick_columns(orbitals, flat, grid_base, rows).astype(jnp.float32).astype(jnp.bfloat16),
+            "grid",
+        ),
+        axis=0,
     )
     whole = lax.all_gather(local_pivots, "orb", axis=0, tiled=True)
     pivot_pairs = contract_first(whole, whole)

time: 282 us -> 265 us (0.940)
  waiting for transfers between devices: 80.1 us -> 61.1 us
    psum x1 -> x0, waiting for transfers between devices: 74.2 us -> none  [on_device(): lax.psum(pick_columns(orbitals, flat, grid_base, rows).astype(jnp.float32...]
    all_gather x0 -> x1, waiting for transfers between devices: none -> 54.6 us  [on_device(): lax.all_gather(pick_columns(orbitals, flat, grid_base, rows).astype(jnp.f...]
    unnamed x14 -> x12, local copies, waits for them, and re-layouts: 15.5 us -> 14.7 us
  transfers between devices with their start and end apart: 4 -> 4, of which waited for: 2 -> 2; matrix products, arithmetic and copies ran while one was open for 31% -> 33% of each run, Pallas kernels for 0% -> 0%
where the time goes in v1:
time: 265 us; the launch traced here: 264 us
  other arithmetic  67.6 us (26%)
  blocking collectives  62.5 us (24%)
  waiting for transfers between devices  61.1 us (23%)
  matrix products  34.6 us (13%)
  local copies, waits for them, and re-layouts  22.9 us (9%)
  between operations  14.8 us (6%)
    all_gather x1, waiting for transfers between devices, on_device(): lax.all_gather(pick_columns(orbitals, flat, grid_base, rows).astype(jnp.f...  54.6 us
    pmax x1, blocking collectives, on_device(): peaks.append(lax.pmax(jnp.max(diagonal), ('grid', 'orb')))  39.5 us
    another operation x9, other arithmetic, on_device(): lower = jnp.linalg.cholesky(block)  28.5 us
    another operation x6, other arithmetic, on_device(): fresh = jax.scipy.linalg.solve_triangular(lower, columns.T, lower=True).T  24 us
    dot_general x4, matrix products, contract_first(): lax.dot_general(left, right, (((0,), (0,)), ((), ())), preferred_element_...  20.2 us
    unnamed x12, local copies, waits for them, and re-layouts  14.7 us
    unnamed x1, blocking collectives  12.3 us
    all_gather x1, blocking collectives, on_device(): whole = lax.all_gather(local_pivots, 'orb', axis=0, tiled=True)  10.7 us
  transfers between devices with their start and end apart: 4, of which 2 were waited for; matrix products, arithmetic and copies ran while one was open for 33% of the time, Pallas kernels for 0%

profile of v1, /device:TPU:0, one launch (start us, length us, event | category | flops | bytes accessed | tf_op | source)
XLA Modules:
  0.0 263.7 jit_solution(13357998127385898650)
XLA Ops:
  8.8 11.6 %copy.36 = bf16[450,8192]{0,1:T(8,128)(2,1)} copy(bf16[450,8192]{1,0:T(8,128)(2,1)} %param.17) | data formatting | bytes 14745600 | tf_op args[0]
  20.5 6.5 %gather_fusion = bf16[288,450]{1,0:T(8,128)(2,1)S(1)} fusion(bf16[450,8192]{0,1:T(8,128)(2,1)} %copy.36, s32[1024]{0:T(1024)S(1)} %pad_clamp_fusion), kind=kCustom, calls=%fused_computation | custom fusion | bytes 519552 | tf_op jit(solution)/shard_map/jit(_take)/gather | solution.py:12
  27.0 0.9 fusion.12
  27.9 54.6 %all-gather.3.cloned.1.call-done = bf16[8,450,288]{1,2,0:T(8,128)(2,1)} async-done(((bf16[1,450,288]{1,2,0:T(8,128)(2,1)}), bf16[8,450,288]{1,2,0:T(8,128)(2,1)}) %all-gather.3.cloned.1.call-update) | async-done | bytes 2073616 | tf_op jit(solution)/shard_map/all_gather | solution.py:40
  82.6 2.1 reduce_sum.48
  84.7 6.3 %convolution_bitcast_fusion.2 = f32[8192,96]{0,1:T(8,128)} fusion(bf16[450,8192]{1,0:T(8,128)(2,1)} %param.17, bf16[450,288]{0,1:T(8,128)(2,1)S(1)} %reduce_sum.48), kind=kOutput, calls=%fused_computation.4 | convolution fusion | flops 707788800 | bytes 10616832 | tf_op jit(solution)/shard_map/dot_general | solution.py:17
  91.1 6.3 %convolution_bitcast_fusion.1 = f32[8192,96]{0,1:T(8,128)} fusion(bf16[450,8192]{1,0:T(8,128)(2,1)} %param.17, bf16[450,288]{0,1:T(8,128)(2,1)S(1)} %reduce_sum.48), kind=kOutput, calls=%fused_computation.3 | convolution fusion | flops 707788800 | bytes 10616832 | tf_op jit(solution)/shard_map/dot_general | solution.py:17
  97.5 6.8 %convolution_bitcast_fusion = f32[8192,96]{0,1:T(8,128)} fusion(bf16[450,8192]{1,0:T(8,128)(2,1)} %param.17, bf16[450,288]{0,1:T(8,128)(2,1)S(1)} %reduce_sum.48), kind=kOutput, calls=%fused_computation.2 | convolution fusion | flops 707788800 | bytes 10616832 | tf_op jit(solution)/shard_map/dot_general | solution.py:17
  107.5 4.8 %multiply_reduce_fusion = f32[8192]{0:T(1024)S(1)} fusion(bf16[450,8192]{1,0:T(8,128)(2,1)} %param.17), kind=kLoop, calls=%fused_computation.1 | loop fusion | flops 11051008 | bytes 7405568 | tf_op jit(solution)/shard_map/reduce_sum | solution.py:31
  112.3 12.3 %all-reduce.2 = f32[8192]{0:T(1024)S(1)} all-reduce(f32[8192]{0:T(1024)S(1)} %multiply_reduce_fusion), channel_id=5, replica_groups=mesh['grid'=8,'orb'=4] {'orb'}, use_global_device_ids=true, to_apply=%region_9.13.clone | all-reduce | flops 8192 | bytes 65536
  124.6 10.7 %all-gather = bf16[4,450,288]{1,2,0:T(8,128)(2,1)S(1)} all-gather(bf16[1,450,288]{1,2,0:T(8,128)(2,1)S(1)} %bitcast.95), channel_id=1, replica_groups=mesh['grid'=8,'orb'=4] {'orb'}, dimensions={0}, use_global_device_ids=true | all-gather | bytes 1296000 | tf_op jit(solution)/shard_map/all_gather | solution.py:46
  135.3 0.9 copy.37
  136.2 1.6 reshape.247
  137.8 0.8 fusion.55
  139.2 8.8 %cholesky.59 = f32[96,96]{1,0:T(8,128)S(1)} custom-call(f32[96,96]{1,0:T(8,128)S(1)} %fusion.37), custom_call_target="Cholesky" | custom-call | tf_op jit(solution)/shard_map/jit(cholesky)/cholesky | solution.py:71
  149.3 7.4 %custom-call.11 = f32[1,96,96]{1,2,0:T(8,128)S(1)} custom-call(f32[1,96,96]{2,1,0:T(8,128)S(1)} %fusion.26), custom_call_target="InvertDiagBlocksLowerTriangular" | custom-call | tf_op jit(solution)/shard_map/jit(_solve_triangular)/triangular_solve | solution.py:72
  156.7 1.0 fusion.5
  158.3 8.8 %cholesky.70 = f32[96,96]{1,0:T(8,128)S(1)} custom-call(f32[96,96]{1,0:T(8,128)S(1)} %fusion.34), custom_call_target="Cholesky" | custom-call | tf_op jit(solution)/shard_map/jit(cholesky)/cholesky | solution.py:71
  168.4 7.4 %custom-call.13 = f32[1,96,96]{1,2,0:T(8,128)S(1)} custom-call(f32[1,96,96]{2,1,0:T(8,128)S(1)} %fusion.27), custom_call_target="InvertDiagBlocksLowerTriangular" | custom-call | tf_op jit(solution)/shard_map/jit(_solve_triangular)/triangular_solve | solution.py:72
  176.5 1.0 fusion.4
  178.2 8.9 %cholesky.81 = f32[96,96]{1,0:T(8,128)S(1)} custom-call(f32[96,96]{1,0:T(8,128)S(1)} %fusion.30), custom_call_target="Cholesky" | custom-call | tf_op jit(solution)/shard_map/jit(cholesky)/cholesky | solution.py:71
  188.4 7.4 %custom-call.15 = f32[1,96,96]{1,2,0:T(8,128)S(1)} custom-call(f32[1,96,96]{2,1,0:T(8,128)S(1)} %fusion.28), custom_call_target="InvertDiagBlocksLowerTriangular" | custom-call | tf_op jit(solution)/shard_map/jit(_solve_triangular)/triangular_solve | solution.py:72
  195.8 2.6 %multiply_reduce_fusion.3 = (f32[2048]{0:T(1024)S(1)}, f32[2048,96]{0,1:T(8,128)S(1)}) fusion(pred[]{:T(512)} %compare_reduce_fusion.4, f32[2048,96]{0,1:T(8,128)} %reduce-scatter.4.cloned.1.call-done, f32[1,96,96]{1,2,0:T(8,128)S(1)} %custom-call.11), kind=kOutput, calls=%fused_computation.25 | convolution fusion | flops 227473408 | bytes 1617921 | tf_op jit(solution)/shard_map/jit(_solve_triangular)/triangular_solve | solution.py:72
  198.8 2.3 fusion.1
  201.1 1.5 bitcast_dynamic-update-slice_fusion
  202.7 6.3 %reduce-scatter.8.cloned.1.call-done = f32[2048,96]{0,1:T(8,128)} async-done(((f32[8192,96]{0,1:T(8,128)}), f32[2048,96]{0,1:T(8,128)}) %reduce-scatter.8.cloned.1.call-update) | async-done | bytes 786448 | tf_op jit(solution)/shard_map/reduce_scatter | solution.py:61
  209.0 3.3 %fusion = f32[96,2048]{1,0:T(8,128)S(1)} fusion(f32[2048,288]{0,1:T(8,128)S(1)} %get-tuple-element.81, f32[2048,96]{0,1:T(8,128)} %reduce-scatter.8.cloned.1.call-done, f32[288,288]{0,1:T(8,128)} %copy-done.1), kind=kOutput, calls=%fused_computation.7 | convolution fusion | flops 680067072 | bytes 4079616 | tf_op jit(solution)/shard_map/dot_general | solution.py:68
  212.3 0.9 multiply_reduce_fusion.1
  213.2 0.8 fusion.47
  214.0 1.2 fusion.49
  215.2 39.5 %all-reduce.3 = (f32[1]{0:T(128)}, f32[1]{0:T(128)}, f32[1]{0:T(128)}) all-reduce(f32[1]{0:T(128)} %bitcast.31, f32[1]{0:T(128)} %bitcast.30, f32[1]{0:T(128)} %bitcast.29), channel_id=1, replica_groups=mesh['grid'=8,'orb'=4] {'grid','orb'}, use_global_device_ids=true, to_apply=%region_18.22 | all-reduce | flops 3 | bytes 24 | tf_op jit(solution)/shard_map/pmax | solution.py:80
  254.7 2.5 pad_maximum_fusion
  (53 shorter events, 11.2 us)
Async XLA Ops:
  7.2 75.4 %all-gather.3.cloned.1.call-start = ((), (), s32[]{:S(2)}) async-start(), calls=%async_computation.3 | async-start | bytes 2654208 | tf_op jit(solution)/shard_map/all_gather | solution.py:40
  27.9 167.9 %reduce-scatter.4.cloned.1.call-start = ((), (), s32[]{:S(2)}) async-start(), calls=%async_computation.4 | async-start | bytes 3932160 | tf_op jit(solution)/shard_map/reduce_scatter | solution.py:61
  91.0 107.7 %reduce-scatter.6.cloned.1.call-start = ((), (), s32[]{:S(2)}) async-start(), calls=%async_computation.5 | async-start | bytes 3932160 | tf_op jit(solution)/shard_map/reduce_scatter | solution.py:61
  97.4 111.5 %reduce-scatter.8.cloned.1.call-start = ((), (), s32[]{:S(2)}) async-start(), calls=%async_computation.6 | async-start | bytes 3932160 | tf_op jit(solution)/shard_map/reduce_scatter | solution.py:61
  104.3 0.7 copy-start.2
  177.5 21.0 %copy-start.1 = (f32[288,288]{0,1:T(8,128)}, f32[288,288]{0,1:T(8,128)S(1)}, u32[]{:S(2)}) copy-start(f32[288,288]{0,1:T(8,128)S(1)} %fusion.4) | copy-start | bytes 995332
  213.2 44.0 %copy-start = (f32[2048,288]{0,1:T(8,128)}, f32[2048,288]{0,1:T(8,128)S(1)}, u32[]{:S(2)}) copy-start(f32[2048,288]{0,1:T(8,128)S(1)} %get-tuple-element.77) | copy-start | bytes 7077892
Sparse Core Ops, SparseCore 0:
  28.0 54.5 all-gather.2
  91.2 36.7 reduce-scatter.3
  130.5 38.0 reduce-scatter.5
  171.1 37.8 reduce-scatter.7
